TPU v7x, 32 devices: a whole 2x2x4 slice. The times are simulated.
32 devices in a mesh: rep: 2 (over x), ep: 16 (over z, y, core).
Axes of the slice: x: 2, y: 2, z: 4, core: 2. Of those that a mesh axis runs over, the one named last changes fastest.
Arguments:
- forward_tokens: bfloat16 [2048, 1024], P(('rep', 'ep')), parts along dimension 0, may hold values from -6 to 6
- forward_ids: int32 [2048, 6], P(('rep', 'ep')), parts along dimension 0, may hold values from 0 to 15, all different within a row; in each aligned block of 64 rows (0 to 63, 64 to 127, ...) at most 32 rows name the same one
- forward_mix: float32 [2048, 6], P(('rep', 'ep')), parts along dimension 0, may hold values from 0.1 to 1
- backward_tokens: bfloat16 [2048, 1024], P(('rep', 'ep')), parts along dimension 0, may hold values from -6 to 6
- backward_ids: int32 [2048, 6], P(('rep', 'ep')), parts along dimension 0, may hold values from 0 to 15, all different within a row; in each aligned block of 64 rows (0 to 63, 64 to 127, ...) at most 32 rows name the same one
- backward_mix: float32 [2048, 6], P(('rep', 'ep')), parts along dimension 0, may hold values from 0.1 to 1
- backward_grad: bfloat16 [2048, 1024], P(('rep', 'ep')), parts along dimension 0, may hold values from -6 to 6
- gate_weight: bfloat16 [32, 1024, 704], P(('rep', 'ep')), parts along dimension 0, may hold values from -0.1875 to 0.1875
- up_weight: bfloat16 [32, 1024, 704], P(('rep', 'ep')), parts along dimension 0, may hold values from -0.1875 to 0.1875
- down_weight: bfloat16 [32, 704, 1024], P(('rep', 'ep')), parts along dimension 0, may hold values from -0.21875 to 0.21875
Outputs:
- forward_out: bfloat16 [2048, 1024], P(('rep', 'ep')), parts along dimension 0
- input_grad: bfloat16 [2048, 1024], P(('rep', 'ep')), parts along dimension 0
There are 2 independent parts, one for each index of `rep`. A program takes and returns all parts, laid end to end along the dimension named above; each array names one. Nothing has to cross between parts.
Inputs may be any that keep to these rules, and one draw needn't show every extreme that they name: `forward_ids`: each row names 6 different experts. `forward_ids`: among the 64 rows of one token owner no expert is named more than 32 times, a bound that some block reaches. `backward_ids`: each row names 6 different experts. `backward_ids`: among the 64 rows of one token owner no expert is named more than 32 times, a bound that some block reaches.
All inputs are finite; a program needn't handle non-finite values.
Results may differ from a plain program's by a relative error of at most 0.0058.
Values may be sent and summed in bfloat16 or wider, within the bound.
A program may use at most 64 MiB of HBM per device.

v0:
```python
import jax
import jax.numpy as jnp
from jax import lax
from jax.sharding import PartitionSpec as P


def expert_forward(expert_rows, gate_matrix, up_matrix, down_matrix):
    gate_pre = jnp.dot(expert_rows, gate_matrix, preferred_element_type=jnp.float32)
    up_pre = jnp.dot(expert_rows, up_matrix, preferred_element_type=jnp.float32)
    hidden = (gate_pre * jax.nn.sigmoid(gate_pre) * up_pre).astype(jnp.bfloat16)
    return jnp.dot(hidden, down_matrix, preferred_element_type=jnp.float32).astype(jnp.bfloat16)


def expert_backward(expert_rows, row_grads, gate_matrix, up_matrix, down_matrix):
    gate_pre = jnp.dot(expert_rows, gate_matrix, preferred_element_type=jnp.float32)
    up_pre = jnp.dot(expert_rows, up_matrix, preferred_element_type=jnp.float32)
    sigmoid_gate = jax.nn.sigmoid(gate_pre)
    hidden_grad = jnp.dot(row_grads, down_matrix.T, preferred_element_type=jnp.float32)
    gate_grad = (
        hidden_grad * up_pre * sigmoid_gate * (1.0 + gate_pre * (1.0 - sigmoid_gate))
    ).astype(jnp.bfloat16)
    up_grad = (hidden_grad * gate_pre * sigmoid_gate).astype(jnp.bfloat16)
    rows_grad = jnp.dot(gate_grad, gate_matrix.T, preferred_element_type=jnp.float32)
    rows_grad = rows_grad + jnp.dot(up_grad, up_matrix.T, preferred_element_type=jnp.float32)
    return rows_grad.astype(jnp.bfloat16)


def route_targets(expert_ids, experts, capacity):
    tok_rows, chosen = expert_ids.shape
    flat_ids = expert_ids.reshape(tok_rows * chosen)
    onehot = (flat_ids[:, None] == jnp.arange(experts, dtype=jnp.int32)[None, :]).astype(jnp.int32)
    before = jnp.cumsum(onehot, axis=0) - onehot
    slot_index = jnp.sum(before * onehot, axis=1)
    return (flat_ids * capacity + slot_index).reshape(tok_rows, chosen)


def dispatch_rows(targets, experts, capacity, sources):
    places = jnp.arange(experts * capacity, dtype=jnp.int32)
    picker = jnp.any(targets[None, :, :] == places[:, None, None], axis=2).astype(jnp.bfloat16)
    return tuple(
        (
            jnp.dot(picker, values, preferred_element_type=jnp.float32)
            .astype(jnp.bfloat16)
            .reshape(experts, capacity, values.shape[1])
            for values in sources
        )
    )


def combine_rows(returned, targets, mixing):
    flat_rows = returned.reshape(returned.shape[0] * returned.shape[1], returned.shape[2])
    picked = flat_rows[targets].astype(jnp.float32)
    return jnp.sum(mixing[:, :, None] * picked, axis=1).astype(jnp.bfloat16)


def run_experts(received, apply, gate_weight, up_weight, down_weight):
    senders = lax.axis_size("ep")
    local_count = gate_weight.shape[0]
    slot_count = received[0].shape[1]
    feature_width = received[0].shape[2]
    expert_rows = tuple(
        (
            values.reshape(senders, local_count, slot_count, feature_width)[:, 0].reshape(
                senders * slot_count, feature_width
            )
            for values in received
        )
    )
    result = apply(expert_rows, gate_weight[0], up_weight[0], down_weight[0])
    outputs = [result.reshape(senders, slot_count, feature_width)]
    return jnp.stack(outputs, axis=1).reshape(senders * local_count, slot_count, feature_width)


def apply_forward(expert_rows, gate_matrix, up_matrix, down_matrix):
    return expert_forward(expert_rows[0], gate_matrix, up_matrix, down_matrix)


def apply_backward(expert_rows, gate_matrix, up_matrix, down_matrix):
    return expert_backward(expert_rows[0], expert_rows[1], gate_matrix, up_matrix, down_matrix)


def per_device(
    forward_tokens,
    forward_ids,
    forward_mix,
    backward_tokens,
    backward_ids,
    backward_mix,
    backward_grad,
    gate_weight,
    up_weight,
    down_weight,
):
    tok_rows, chosen = forward_ids.shape
    experts = lax.axis_size("ep") * gate_weight.shape[0]
    capacity = tok_rows * chosen * 4 // (3 * experts)
    targets_forward = route_targets(forward_ids, experts, capacity)
    targets_backward = route_targets(backward_ids, experts, capacity)
    (sent_forward,) = dispatch_rows(targets_forward, experts, capacity, (forward_tokens,))
    sent_backward, sent_grads = dispatch_rows(
        targets_backward, experts, capacity, (backward_tokens, backward_grad)
    )
    outputs_forward = run_experts(
        (lax.all_to_all(sent_forward, "ep", split_axis=0, concat_axis=0, tiled=True),),
        apply_forward,
        gate_weight,
        up_weight,
        down_weight,
    )
    back_forward = lax.all_to_all(outputs_forward, "ep", split_axis=0, concat_axis=0, tiled=True)
    outputs_backward = run_experts(
        (
            lax.all_to_all(sent_backward, "ep", split_axis=0, concat_axis=0, tiled=True),
            lax.all_to_all(sent_grads, "ep", split_axis=0, concat_axis=0, tiled=True),
        ),
        apply_backward,
        gate_weight,
        up_weight,
        down_weight,
    )
    back_backward = lax.all_to_all(outputs_backward, "ep", split_axis=0, concat_axis=0, tiled=True)
    forward_out = combine_rows(back_forward, targets_forward, forward_mix)
    input_grad = combine_rows(back_backward, targets_backward, backward_mix)
    return (forward_out, input_grad)


def solution(mesh):
    in_specs = (
        P(("rep", "ep"), None),
        P(("rep", "ep"), None),
        P(("rep", "ep"), None),
        P(("rep", "ep"), None),
        P(("rep", "ep"), None),
        P(("rep", "ep"), None),
        P(("rep", "ep"), None),
        P(("rep", "ep"), None, None),
        P(("rep", "ep"), None, None),
        P(("rep", "ep"), None, None),
    )
    out_specs = (P(("rep", "ep"), None), P(("rep", "ep"), None))
    return jax.shard_map(
        per_device, mesh=mesh, in_specs=in_specs, out_specs=out_specs, check_vma=False
    )
```

profile of v0, /device:TPU:0, one launch (start us, length us, event | category | flops | bytes accessed | tf_op | source)
XLA Modules:
  0.0 164.8 jit_solution(8234813588181878833)
XLA Ops:
  0.6 0.9 copy.49
  4.2 2.5 %convolution_convert_fusion = bf16[512,1024]{1,0:T(8,128)(2,1)} fusion(pred[512,64]{0,1:T(8,128)(4,1)S(1)} %fusion.25, bf16[64,1024]{1,0:T(8,128)(2,1)} %param.13), kind=kOutput, calls=%fused_computation.5 | convolution fusion | flops 67633152 | bytes 1212416 | tf_op jit(solution)/shard_map/dot_general | solution.py:42
  6.6 7.4 %all-to-all-start.3 = ((bf16[16,32,1024]{2,1,0:T(8,128)(2,1)}), bf16[16,32,1024]{2,1,0:T(8,128)(2,1)S(1)}, u32[]{:S(2)}, u32[]{:S(2)}) async-start(bf16[16,32,1024]{2,1,0:T(8,128)(2,1)} %bitcast.11), calls=%async_computation.3 | async-start | bytes 2097152 | tf_op jit(solution)/shard_map/all_to_all | solution.py:113
  14.1 1.5 convolution_convert_fusion.1
  15.5 21.4 %all-to-all-done.3 = bf16[16,32,1024]{2,1,0:T(8,128)(2,1)S(1)} async-done(((bf16[16,32,1024]{2,1,0:T(8,128)(2,1)}), bf16[16,32,1024]{2,1,0:T(8,128)(2,1)S(1)}, u32[]{:S(2)}, u32[]{:S(2)}) %all-to-all-start.3) | async-done | bytes 1048608 | tf_op jit(solution)/shard_map/all_to_all | solution.py:113
  36.9 6.8 %all-to-all-start.2 = ((bf16[16,32,1024]{2,1,0:T(8,128)(2,1)}), bf16[16,32,1024]{2,1,0:T(8,128)(2,1)S(1)}, u32[]{:S(2)}, u32[]{:S(2)}) async-start(bf16[16,32,1024]{2,1,0:T(8,128)(2,1)} %bitcast.9), calls=%async_computation.2 | async-start | bytes 2097152 | tf_op jit(solution)/shard_map/all_to_all | solution.py:114
  44.4 0.9 eq.80
  45.3 0.9 eq.76
  46.9 2.6 %reduce-window.14 = s32[16,3,128]{2,0,1:T(8,128)} reduce-window(s32[16,3,128]{2,0,1:T(8,128)} %fusion.35, s32[]{:T(128)} %constant.7.clone.1), window={size=1x1x128 pad=0_0x0_0x127_0}, to_apply=%region_0.0 | reduce-window | flops 780288 | bytes 49156 | tf_op jit(solution)/shard_map/reduce-window
  49.4 0.9 slice_reduce_fusion.1
  53.6 2.4 %convolution_convert_fusion.3 = bf16[512,1024]{1,0:T(8,128)(2,1)} fusion(pred[512,64]{0,1:T(8,128)(4,1)S(1)} %fusion.24, bf16[64,1024]{1,0:T(8,128)(2,1)} %param.10), kind=kOutput, calls=%fused_computation.8 | convolution fusion | flops 67633152 | bytes 1212416 | tf_op jit(solution)/shard_map/dot_general | solution.py:42
  55.9 10.7 %all-to-all-done.2 = bf16[16,32,1024]{2,1,0:T(8,128)(2,1)S(1)} async-done(((bf16[16,32,1024]{2,1,0:T(8,128)(2,1)}), bf16[16,32,1024]{2,1,0:T(8,128)(2,1)S(1)}, u32[]{:S(2)}, u32[]{:S(2)}) %all-to-all-start.2) | async-done | bytes 1048608 | tf_op jit(solution)/shard_map/all_to_all | solution.py:114
  66.6 6.8 %all-to-all-start = ((bf16[16,32,1024]{2,1,0:T(8,128)(2,1)}), bf16[16,32,1024]{2,1,0:T(8,128)(2,1)}, u32[]{:S(2)}, u32[]{:S(2)}) async-start(bf16[16,32,1024]{2,1,0:T(8,128)(2,1)} %bitcast.1), calls=%async_computation | async-start | bytes 2097152 | tf_op jit(solution)/shard_map/all_to_all | solution.py:104
  73.5 3.5 %fusion.10 = f32[512,704]{0,1:T(8,128)} fusion(bf16[512,1024]{1,0:T(8,128)(2,1)S(1)} %bitcast.90, bf16[1,1024,704]{1,2,0:T(8,128)(2,1)} %param.17), kind=kOutput, calls=%fused_computation.21 | convolution fusion | flops 738197504 | bytes 3932160 | tf_op jit(solution)/shard_map/dot_general | solution.py:15
  77.0 2.1 %fusion.2 = f32[512,704]{0,1:T(8,128)} fusion(bf16[512,1024]{1,0:T(8,128)(2,1)S(1)} %bitcast.92, bf16[1,704,1024]{2,1,0:T(8,128)(2,1)S(1)} %copy-done.5), kind=kOutput, calls=%fused_computation.13 | convolution fusion | flops 738197504 | bytes 3932160 | tf_op jit(solution)/shard_map/dot_general | solution.py:18
  79.1 5.7 %fusion.8 = f32[512,1024]{1,0:T(8,128)} fusion(bf16[1,1024,704]{1,2,0:T(8,128)(2,1)} %param.17, f32[512,704]{0,1:T(8,128)} %fusion.10, f32[512,704]{0,1:T(8,128)} %fusion.2, bf16[512,1024]{1,0:T(8,128)(2,1)S(1)} %bitcast.91, bf16[1,1024,704]{1,2,0:T(8,128)(2,1)S(1)} %copy-done), kind=kOutput, calls=%fused_computation.19 | convolution fusion | flops 1479999488 | bytes 8912896 | tf_op jit(solution)/shard_map/dot_general | solution.py:23
  84.7 4.5 %add_convert_fusion = bf16[512,1024]{1,0:T(8,128)(2,1)} fusion(f32[512,1024]{1,0:T(8,128)} %fusion.8, bf16[1,1024,704]{1,2,0:T(8,128)(2,1)S(1)} %copy-done, f32[512,704]{0,1:T(8,128)} %fusion.2, f32[512,704]{0,1:T(8,128)} %fusion.10), kind=kOutput, calls=%fused_computation.3 | convolution fusion | flops 741408768 | bytes 7471104 | tf_op jit(solution)/shard_map/dot_general | solution.py:24
  89.2 7.2 %all-to-all-done = bf16[16,32,1024]{2,1,0:T(8,128)(2,1)} async-done(((bf16[16,32,1024]{2,1,0:T(8,128)(2,1)}), bf16[16,32,1024]{2,1,0:T(8,128)(2,1)}, u32[]{:S(2)}, u32[]{:S(2)}) %all-to-all-start) | async-done | bytes 1048608 | tf_op jit(solution)/shard_map/all_to_all | solution.py:104
  96.4 6.8 %all-to-all-start.4 = ((bf16[16,32,1024]{2,1,0:T(8,128)(2,1)}), bf16[16,32,1024]{2,1,0:T(8,128)(2,1)S(1)}, u32[]{:S(2)}, u32[]{:S(2)}) async-start(bf16[16,32,1024]{2,1,0:T(8,128)(2,1)} %bitcast.13), calls=%async_computation.4 | async-start | bytes 2097152 | tf_op jit(solution)/shard_map/all_to_all | solution.py:121
  103.2 3.7 %fusion.12 = f32[512,704]{0,1:T(8,128)} fusion(bf16[512,1024]{1,0:T(8,128)(2,1)} %bitcast.2, bf16[1,1024,704]{1,2,0:T(8,128)(2,1)} %param.17), kind=kOutput, calls=%fused_computation.23 | convolution fusion | flops 738197504 | bytes 3932160 | tf_op jit(solution)/shard_map/dot_general | solution.py:8
  106.9 4.9 %convolution_convert_fusion.2 = bf16[512,1024]{1,0:T(8,128)(2,1)} fusion(bf16[1,704,1024]{2,1,0:T(8,128)(2,1)} %param.19, bf16[512,1024]{1,0:T(8,128)(2,1)} %bitcast.2, bf16[1,1024,704]{1,2,0:T(8,128)(2,1)S(1)} %copy-done, f32[512,704]{0,1:T(8,128)} %fusion.12), kind=kOutput, calls=%fused_computation.7 | convolution fusion | flops 1479081984 | bytes 6422528 | tf_op jit(solution)/shard_map/dot_general | solution.py:11
  111.9 14.2 %all-to-all-done.4 = bf16[16,32,1024]{2,1,0:T(8,128)(2,1)S(1)} async-done(((bf16[16,32,1024]{2,1,0:T(8,128)(2,1)}), bf16[16,32,1024]{2,1,0:T(8,128)(2,1)S(1)}, u32[]{:S(2)}, u32[]{:S(2)}) %all-to-all-start.4) | async-done | bytes 1048608 | tf_op jit(solution)/shard_map/all_to_all | solution.py:121
  126.1 6.8 %all-to-all-start.1 = ((bf16[16,32,1024]{2,1,0:T(8,128)(2,1)}), bf16[16,32,1024]{2,1,0:T(8,128)(2,1)S(1)}, u32[]{:S(2)}, u32[]{:S(2)}) async-start(bf16[16,32,1024]{2,1,0:T(8,128)(2,1)} %bitcast.93), calls=%async_computation.1 | async-start | bytes 2097152 | tf_op jit(solution)/shard_map/all_to_all | solution.py:110
  133.6 0.9 reshape.90
  135.2 0.9 reshape.82
  136.8 1.4 copy.48
  138.2 2.7 %gather_fusion.1 = bf16[384,1024]{1,0:T(8,128)(2,1)} fusion(bf16[512,1024]{1,0:T(8,128)(2,1)S(1)} %bitcast.88, s32[1024]{0:T(1024)S(1)} %pad_clamp_fusion), kind=kCustom, calls=%fused_computation.1 | custom fusion | bytes 1574400 | tf_op jit(solution)/shard_map/gather | solution.py:52
  140.9 2.5 %reshape.101 = f32[64,6,1024]{2,1,0:T(8,128)} reshape(bf16[384,1024]{1,0:T(8,128)(2,1)} %gather_fusion.1) | data formatting | bytes 2359296 | tf_op jit(solution)/shard_map/convert_element_type | solution.py:52
  143.4 12.4 %all-to-all-done.1 = bf16[16,32,1024]{2,1,0:T(8,128)(2,1)S(1)} async-done(((bf16[16,32,1024]{2,1,0:T(8,128)(2,1)}), bf16[16,32,1024]{2,1,0:T(8,128)(2,1)S(1)}, u32[]{:S(2)}, u32[]{:S(2)}) %all-to-all-start.1) | async-done | bytes 1048608 | tf_op jit(solution)/shard_map/all_to_all | solution.py:110
  155.8 2.7 %gather_fusion = bf16[384,1024]{1,0:T(8,128)(2,1)} fusion(bf16[512,1024]{1,0:T(8,128)(2,1)S(1)} %bitcast.89, s32[1024]{0:T(1024)S(1)} %pad_clamp_fusion.1), kind=kCustom, calls=%fused_computation | custom fusion | bytes 1574400 | tf_op jit(solution)/shard_map/gather | solution.py:52
  158.5 2.6 %reshape.100 = f32[64,6,1024]{2,1,0:T(8,128)} reshape(bf16[384,1024]{1,0:T(8,128)(2,1)} %gather_fusion) | data formatting | bytes 2359296 | tf_op jit(solution)/shard_map/convert_element_type | solution.py:52
  161.1 3.7 %multiply_reduce_fusion = (bf16[64,1024]{1,0:T(8,128)(2,1)}, bf16[64,1024]{1,0:T(8,128)(2,1)}) fusion(f32[64,6,1024]{2,1,0:T(8,128)S(1)} %copy-done.1, f32[64,6]{1,0:T(8,128)} %copy.48, f32[64,6,1024]{2,1,0:T(8,128)} %reshape.100, f32[64,6]{1,0:T(8,128)} %copy.42), kind=kLoop, calls=%fused_computation.2 | loop fusion | flops 1441792 | bytes 3410944 | tf_op jit(solution)/shard_map/reduce_sum | solution.py:53
  (36 shorter events, 9.3 us)
Async XLA Ops:
  0.6 78.4 %copy-start = (bf16[1,1024,704]{1,2,0:T(8,128)(2,1)S(1)}, bf16[1,1024,704]{1,2,0:T(8,128)(2,1)}, u32[]{:S(2)}) copy-start(bf16[1,1024,704]{1,2,0:T(8,128)(2,1)} %param.18) | copy-start | bytes 4325380
  4.1 9.9 %copy-start.2 = (bf16[64,1024]{1,0:T(8,128)(2,1)S(1)}, bf16[64,1024]{1,0:T(8,128)(2,1)}, u32[]{:S(2)}) copy-start(bf16[64,1024]{1,0:T(8,128)(2,1)} %param.16) | copy-start | bytes 393220
  6.6 30.3 %all-to-all-start.3 = ((bf16[16,32,1024]{2,1,0:T(8,128)(2,1)}), bf16[16,32,1024]{2,1,0:T(8,128)(2,1)S(1)}, u32[]{:S(2)}, u32[]{:S(2)}) async-start(bf16[16,32,1024]{2,1,0:T(8,128)(2,1)} %bitcast.11), calls=%async_computation.3 | async-start | bytes 2097152 | tf_op jit(solution)/shard_map/all_to_all | solution.py:113
  14.1 29.7 %copy-start.3 = (s32[64,6]{0,1:T(8,128)S(1)}, s32[64,6]{0,1:T(8,128)}, u32[]{:S(2)}) copy-start(s32[64,6]{0,1:T(8,128)} %param.11) | copy-start | bytes 4612
  36.9 29.7 %all-to-all-start.2 = ((bf16[16,32,1024]{2,1,0:T(8,128)(2,1)}), bf16[16,32,1024]{2,1,0:T(8,128)(2,1)S(1)}, u32[]{:S(2)}, u32[]{:S(2)}) async-start(bf16[16,32,1024]{2,1,0:T(8,128)(2,1)} %bitcast.9), calls=%async_computation.2 | async-start | bytes 2097152 | tf_op jit(solution)/shard_map/all_to_all | solution.py:114
  66.6 29.8 %all-to-all-start = ((bf16[16,32,1024]{2,1,0:T(8,128)(2,1)}), bf16[16,32,1024]{2,1,0:T(8,128)(2,1)}, u32[]{:S(2)}, u32[]{:S(2)}) async-start(bf16[16,32,1024]{2,1,0:T(8,128)(2,1)} %bitcast.1), calls=%async_computation | async-start | bytes 2097152 | tf_op jit(solution)/shard_map/all_to_all | solution.py:104
  73.5 3.5 %copy-start.5 = (bf16[1,704,1024]{2,1,0:T(8,128)(2,1)S(1)}, bf16[1,704,1024]{2,1,0:T(8,128)(2,1)}, u32[]{:S(2)}) copy-start(bf16[1,704,1024]{2,1,0:T(8,128)(2,1)} %param.19) | copy-start | bytes 4325380
  96.4 29.7 %all-to-all-start.4 = ((bf16[16,32,1024]{2,1,0:T(8,128)(2,1)}), bf16[16,32,1024]{2,1,0:T(8,128)(2,1)S(1)}, u32[]{:S(2)}, u32[]{:S(2)}) async-start(bf16[16,32,1024]{2,1,0:T(8,128)(2,1)} %bitcast.13), calls=%async_computation.4 | async-start | bytes 2097152 | tf_op jit(solution)/shard_map/all_to_all | solution.py:121
  111.9 24.2 %copy-start.4 = (f32[64,6]{0,1:T(8,128)S(1)}, f32[64,6]{0,1:T(8,128)}, u32[]{:S(2)}) copy-start(f32[64,6]{0,1:T(8,128)} %param.12) | copy-start | bytes 4612
  126.1 29.7 %all-to-all-start.1 = ((bf16[16,32,1024]{2,1,0:T(8,128)(2,1)}), bf16[16,32,1024]{2,1,0:T(8,128)(2,1)S(1)}, u32[]{:S(2)}, u32[]{:S(2)}) async-start(bf16[16,32,1024]{2,1,0:T(8,128)(2,1)} %bitcast.93), calls=%async_computation.1 | async-start | bytes 2097152 | tf_op jit(solution)/shard_map/all_to_all | solution.py:110
  158.5 2.6 %copy-start.1 = (f32[64,6,1024]{2,1,0:T(8,128)S(1)}, f32[64,6,1024]{2,1,0:T(8,128)}, u32[]{:S(2)}) copy-start(f32[64,6,1024]{2,1,0:T(8,128)} %reshape.101) | copy-start | bytes 4718596
where the time goes:
time: 167 us; the launch traced here: 165 us
  waiting for transfers between devices  65.8 us (39%)
  starting transfers between devices  34.6 us (21%)
  matrix products  30.7 us (18%)
  local copies, waits for them, and re-layouts  22.4 us (13%)
  other arithmetic  10.4 us (6%)
    all_to_all x1, waiting for transfers between devices, per_device(): lax.all_to_all(sent_backward, 'ep', split_axis=0, concat_axis=0, tiled=True)  21.4 us
    all_to_all x1, waiting for transfers between devices, per_device(): lax.all_to_all(outputs_backward, 'ep', split_axis=0, concat_axis=0, tiled...  14.2 us
    all_to_all x1, waiting for transfers between devices, per_device(): lax.all_to_all(outputs_forward, 'ep', split_axis=0, concat_axis=0, tiled=...  12.4 us
    all_to_all x1, waiting for transfers between devices, per_device(): lax.all_to_all(sent_grads, 'ep', split_axis=0, concat_axis=0, tiled=True)  10.7 us
    all_to_all x1, starting transfers between devices, per_device(): lax.all_to_all(sent_backward, 'ep', split_axis=0, concat_axis=0, tiled=True)  7.41 us
    all_to_all x1, waiting for transfers between devices, per_device(): lax.all_to_all(sent_forward, 'ep', split_axis=0, concat_axis=0, tiled=True)  7.18 us
    all_to_all x1, starting transfers between devices, per_device(): lax.all_to_all(sent_forward, 'ep', split_axis=0, concat_axis=0, tiled=True)  6.84 us
    all_to_all x1, starting transfers between devices, per_device(): lax.all_to_all(outputs_forward, 'ep', split_axis=0, concat_axis=0, tiled=...  6.8 us
  transfers between devices with their start and end apart: 5, of which 5 were waited for; matrix products, arithmetic and copies ran while one was open for 29% of the time, Pallas kernels for 0%

commit v1 on v0

--- a/solution.py
+++ b/solution.py
@@ -1,6 +1,10 @@
+import functools
+
 import jax
 import jax.numpy as jnp
 from jax import lax
+from jax.experimental import pallas as pl
+from jax.experimental.pallas import tpu as pltpu
 from jax.sharding import PartitionSpec as P
 
 
@@ -124,20 +128,408 @@
     return (forward_out, input_grad)
 
 
+MESH_ID = pl.DeviceIdType.MESH
+RIGHT, LEFT = 0, 1
+TOK_B, GRAD_B, TOK_F, ROUTE = 0, 1, 2, 3
+FWD, BWD = 0, 1
+
+
+def fused_kernel(
+    ep,
+    cap,
+    ft_ref,
+    bt_ref,
+    bg_ref,
+    rt_ref,
+    gate_hbm,
+    up_hbm,
+    down_hbm,
+    of_ref,
+    ob_ref,
+    bt_all,
+    bg_all,
+    ft_all,
+    rt_all,
+    gate,
+    up,
+    down,
+    pick,
+    mixrow,
+    xrows,
+    grows,
+    zrows,
+    pstage,
+    precv,
+    rstage,
+    rrecv,
+    wsem,
+    ag_send,
+    ag_recv,
+    dd_send,
+    dd_recv,
+    ps_send,
+    ps_recv,
+    rs_send,
+    rs_recv,
+):
+    tok, width = ft_ref.shape
+    half = tok // 2
+    ring = ep // 2
+    arm = ring // 2
+    me = lax.axis_index("ep")
+    core = lax.rem(me, 2)
+    quo = me // 2
+    row, col = quo // 2, lax.rem(quo, 2)
+    pos = row + col * (ring - 1 - 2 * row)
+    partner = me + 1 - 2 * core
+
+    def member(offset, which):
+        place = lax.rem(pos + offset + ring, ring)
+        side = place // arm
+        level = place + side * (ring - 1 - 2 * place)
+        return 2 * (2 * level + side) + which
+
+    hop = (member(1, core), member(-1, core))
+    sources = (bt_ref, bg_ref, ft_ref, rt_ref)
+    gathered = (bt_all, bg_all, ft_all, rt_all)
+    started = []
+
+    def remote(src, dst, send, recv, device):
+        return pltpu.make_async_remote_copy(
+            src_ref=src, dst_ref=dst, send_sem=send, recv_sem=recv,
+            device_id={"ep": device}, device_id_type=MESH_ID,
+        )
+
+    def launch(copy):
+        copy.start()
+        started.append(copy)
+
+    barrier = pltpu.get_barrier_semaphore()
+    for other in (hop[0], hop[1], partner):
+        pl.semaphore_signal(barrier, inc=1, device_id={"ep": other}, device_id_type=MESH_ID)
+    pl.semaphore_wait(barrier, 3)
+
+    def owner_at(way, dist, which):
+        return member(-dist if way == RIGHT else dist, which)
+
+    def part(ref, unit, way, dist):
+        if dist == arm and unit != ROUTE:
+            return ref.at[pl.ds(half * way, half)]
+        return ref
+
+    def present(unit, way, dist):
+        return not (unit == ROUTE and dist == arm and way == LEFT)
+
+    def send_on(unit, way, dist):
+        if not present(unit, way, dist):
+            return
+        owner = owner_at(way, dist - 1, core)
+        src = sources[unit] if dist == 1 else gathered[unit].at[owner]
+        dst = gathered[unit].at[owner]
+        launch(remote(part(src, unit, way, dist), part(dst, unit, way, dist),
+                      ag_send.at[unit, way, dist - 1], ag_recv.at[unit, way, dist - 1], hop[way]))
+
+    def await_ring(unit, way, dist):
+        if not present(unit, way, dist):
+            return
+        ref = part(gathered[unit].at[owner_at(way, dist, core)], unit, way, dist)
+        remote(ref, ref, ag_send.at[unit, way, dist - 1], ag_recv.at[unit, way, dist - 1], hop[way]).wait_recv()
+
+    def send_over(unit, way, dist):
+        if not present(unit, way, dist):
+            return
+        owner = owner_at(way, dist, core)
+        src = sources[unit] if dist == 0 else gathered[unit].at[owner]
+        launch(remote(part(src, unit, way, dist), part(gathered[unit].at[owner], unit, way, dist),
+                      dd_send.at[unit, way, dist], dd_recv.at[unit, way, dist], partner))
+
+    def await_over(unit, way, dist):
+        if not present(unit, way, dist):
+            return
+        ref = part(gathered[unit].at[owner_at(way, dist, 1 - core)], unit, way, dist)
+        remote(ref, ref, dd_send.at[unit, way, dist], dd_recv.at[unit, way, dist], partner).wait_recv()
+
+    def begin(units):
+        for unit in units:
+            for way in (RIGHT, LEFT):
+                send_on(unit, way, 1)
+        for unit in units:
+            send_over(unit, RIGHT, 0)
+
+    def forward(units, dist):
+        for unit in units:
+            for way in (RIGHT, LEFT):
+                await_ring(unit, way, dist)
+                if dist < arm:
+                    send_on(unit, way, dist + 1)
+                send_over(unit, way, dist)
+
+    spot = lax.broadcasted_iota(jnp.int32, (cap, tok), 0).astype(jnp.float32)
+    earlier = (
+        lax.broadcasted_iota(jnp.int32, (tok, tok), 0) < lax.broadcasted_iota(jnp.int32, (tok, tok), 1)
+    ).astype(jnp.float32)
+
+    def choose(owner):
+        weights = rt_all[owner, me]
+        chosen = (weights > 0.0).astype(jnp.float32)
+        before = jnp.dot(chosen, earlier, preferred_element_type=jnp.float32)
+        for kind in (FWD, BWD):
+            hit = (spot == before[kind : kind + 1]) & (weights[kind : kind + 1] > 0.0)
+            pick[kind, owner] = hit.astype(jnp.float32).astype(jnp.bfloat16)
+            scale = jnp.sum(jnp.where(hit, weights[kind : kind + 1], 0.0), axis=1, keepdims=True)
+            mixrow[kind, owner] = jnp.broadcast_to(scale, (cap, 128))
+
+    def fetch(kind, owner, source, rows):
+        rows[owner] = jnp.dot(
+            pick[kind, owner], source[owner], preferred_element_type=jnp.float32
+        ).astype(jnp.bfloat16)
+
+    def take(kind, owner):
+        if kind == BWD:
+            choose(owner)
+            fetch(BWD, owner, bt_all, xrows)
+            fetch(BWD, owner, bg_all, grows)
+        else:
+            fetch(FWD, owner, ft_all, xrows)
+
+    def take_ring(kind, dist):
+        take(kind, owner_at(RIGHT, dist, core))
+        if dist < arm:
+            take(kind, owner_at(LEFT, dist, core))
+
+    def take_over(kind, units, dist):
+        ways = (RIGHT,) if dist == 0 else (RIGHT, LEFT)
+        for unit in units:
+            for way in ways:
+                await_over(unit, way, dist)
+        take(kind, owner_at(RIGHT, dist, 1 - core))
+        if 0 < dist < arm:
+            take(kind, owner_at(LEFT, dist, 1 - core))
+
+    span = ep // 2
+
+    def scaled(kind, first, value):
+        scale = mixrow[kind, pl.ds(first, span)].reshape(span * cap, 128)[:, :1]
+        zrows[kind, pl.ds(first, span)] = (value * scale).astype(jnp.bfloat16).reshape(span, cap, width)
+
+    def nt(left, right):
+        return lax.dot_general(left, right, (((1,), (1,)), ((), ())), preferred_element_type=jnp.float32)
+
+    def expert_b(first):
+        x = xrows[pl.ds(first, span)].reshape(span * cap, width)
+        g = grows[pl.ds(first, span)].reshape(span * cap, width)
+        p = jnp.dot(x, gate[...], preferred_element_type=jnp.float32)
+        q = jnp.dot(x, up[...], preferred_element_type=jnp.float32)
+        hidden_grad = nt(g, down[...])
+        s = jax.nn.sigmoid(p)
+        gate_grad = (hidden_grad * q * s * (1.0 + p * (1.0 - s))).astype(jnp.bfloat16)
+        up_grad = (hidden_grad * p * s).astype(jnp.bfloat16)
+        scaled(BWD, first, nt(gate_grad, gate[...]) + nt(up_grad, up[...]))
+
+    def expert_f(first):
+        x = xrows[pl.ds(first, span)].reshape(span * cap, width)
+        p = jnp.dot(x, gate[...], preferred_element_type=jnp.float32)
+        q = jnp.dot(x, up[...], preferred_element_type=jnp.float32)
+        hidden = (p * jax.nn.sigmoid(p) * q).astype(jnp.bfloat16)
+        scaled(FWD, first, jnp.dot(hidden, down[...], preferred_element_type=jnp.float32))
+
+    def contribution(kind, owner):
+        return lax.dot_general(
+            pick[kind, owner], zrows[kind, owner], (((0,), (0,)), ((), ())), preferred_element_type=jnp.float32
+        )
+
+    order = [arm] + [j for d in range(arm - 1, 0, -1) for j in (d, ring - d)] + [0]
+
+    def pair_copy(kind, j):
+        return remote(pstage.at[kind, j], precv.at[kind, j], ps_send.at[kind, j], ps_recv.at[kind, j], partner)
+
+    def hand_over(kind):
+        for j in order:
+            pstage[kind, j] = contribution(kind, member(j, 1 - core)).astype(jnp.bfloat16)
+            launch(pair_copy(kind, j))
+
+    def pair_sum(kind, j):
+        pair_copy(kind, j).wait_recv()
+        return contribution(kind, member(j, core)) + precv[kind, j].astype(jnp.float32)
+
+    def ring_copy(kind, way, step):
+        src, dst = rstage.at[kind, way, step], rrecv.at[kind, way, step]
+        if step == 0:
+            src, dst = src.at[pl.ds(half * way, half)], dst.at[pl.ds(half * way, half)]
+        return remote(src, dst, rs_send.at[kind, way, step], rs_recv.at[kind, way, step], hop[way])
+
+    def reduce_step(kind, step):
+        dist = arm - step
+        if step == 0:
+            value = pair_sum(kind, arm).astype(jnp.bfloat16)
+            for way in (RIGHT, LEFT):
+                rows = pl.ds(half * way, half)
+                rstage[kind, way, 0, rows] = value[half * way : half * way + half]
+                launch(ring_copy(kind, way, 0))
+            return
+        for way in (RIGHT, LEFT):
+            value = pair_sum(kind, dist if way == RIGHT else ring - dist)
+            ring_copy(kind, way, step - 1).wait_recv()
+            if step == 1:
+                for at in (RIGHT, LEFT):
+                    piece = value[half * at : half * at + half]
+                    rows = pl.ds(half * at, half)
+                    if at == way:
+                        piece = piece + rrecv[kind, way, 0, rows].astype(jnp.float32)
+                    rstage[kind, way, 1, rows] = piece.astype(jnp.bfloat16)
+            else:
+                rstage[kind, way, step] = (value + rrecv[kind, way, step - 1].astype(jnp.float32)).astype(
+                    jnp.bfloat16
+                )
+            launch(ring_copy(kind, way, step))
+
+    def finish(kind, out_ref):
+        value = pair_sum(kind, 0)
+        for way in (RIGHT, LEFT):
+            ring_copy(kind, way, arm - 1).wait_recv()
+            value = value + rrecv[kind, way, arm - 1].astype(jnp.float32)
+        out_ref[...] = value.astype(jnp.bfloat16)
+
+    units_b = (ROUTE, TOK_B, GRAD_B)
+    units_f = (TOK_F,)
+    begin(units_b)
+    loads = [
+        pltpu.make_async_copy(hbm.at[0], vmem, wsem.at[i])
+        for i, (hbm, vmem) in enumerate(((gate_hbm, gate), (up_hbm, up), (down_hbm, down)))
+    ]
+    for load in loads:
+        load.start()
+    for unit in range(4):
+        gathered[unit][me] = sources[unit][...]
+    take(BWD, me)
+    for dist in range(1, arm + 1):
+        forward(units_b, dist)
+        if dist == arm - 1:
+            begin(units_f)
+        if dist < arm:
+            take_ring(BWD, dist)
+        take_over(BWD, units_b, dist - 1)
+    take_ring(BWD, arm)
+    take_over(BWD, units_b, arm)
+    for load in loads:
+        load.wait()
+    forward(units_f, 1)
+    expert_b(0)
+    if arm >= 2:
+        forward(units_f, 2)
+    expert_b(span)
+    for dist in range(3, arm + 1):
+        if dist < arm:
+            forward(units_f, dist)
+    hand_over(BWD)
+    reduce_step(BWD, 0)
+    if arm >= 3:
+        forward(units_f, arm)
+    take(FWD, me)
+    for dist in range(1, arm):
+        take_ring(FWD, dist)
+    reduce_step(BWD, 1)
+    take_ring(FWD, arm)
+    for dist in range(0, arm + 1):
+        take_over(FWD, units_f, dist)
+    expert_f(0)
+    for step in range(2, arm - 1):
+        reduce_step(BWD, step)
+    expert_f(span)
+    if arm >= 3:
+        reduce_step(BWD, arm - 1)
+    hand_over(FWD)
+    reduce_step(FWD, 0)
+    finish(BWD, ob_ref)
+    for step in range(1, arm):
+        reduce_step(FWD, step)
+    finish(FWD, of_ref)
+    for copy in started:
+        copy.wait_send()
+
+
+def owner_weights(ids, mix, experts):
+    named = ids[None, :, :] == jnp.arange(experts, dtype=jnp.int32)[:, None, None]
+    return jnp.sum(jnp.where(named, mix[None, :, :], 0.0), axis=2)
+
+
+def per_device_fused(
+    forward_tokens,
+    forward_ids,
+    forward_mix,
+    backward_tokens,
+    backward_ids,
+    backward_mix,
+    backward_grad,
+    gate_weight,
+    up_weight,
+    down_weight,
+):
+    tok, chosen = forward_ids.shape
+    width = forward_tokens.shape[1]
+    ep = lax.axis_size("ep")
+    cap = tok * chosen * 4 // (3 * ep)
+    ring = ep // 2
+    arm = ring // 2
+    bf16, f32 = jnp.bfloat16, jnp.float32
+    route = jnp.stack(
+        [owner_weights(forward_ids, forward_mix, ep), owner_weights(backward_ids, backward_mix, ep)], axis=1
+    )
+    vmem = pl.BlockSpec(memory_space=pltpu.VMEM)
+    hbm = pl.BlockSpec(memory_space=pl.ANY)
+    dma = pltpu.SemaphoreType.DMA
+    return pl.pallas_call(
+        functools.partial(fused_kernel, ep, cap),
+        out_shape=(jax.ShapeDtypeStruct((tok, width), bf16),) * 2,
+        in_specs=[vmem] * 4 + [hbm] * 3,
+        out_specs=(vmem, vmem),
+        scratch_shapes=[pltpu.VMEM((ep, tok, width), bf16)] * 3
+        + [
+            pltpu.VMEM((ep, ep, 2, tok), f32),
+            pltpu.VMEM(gate_weight.shape[1:], bf16),
+            pltpu.VMEM(up_weight.shape[1:], bf16),
+            pltpu.VMEM(down_weight.shape[1:], bf16),
+            pltpu.VMEM((2, ep, cap, tok), bf16),
+            pltpu.VMEM((2, ep, cap, 128), f32),
+            pltpu.VMEM((ep, cap, width), bf16),
+            pltpu.VMEM((ep, cap, width), bf16),
+            pltpu.VMEM((2, ep, cap, width), bf16),
+            pltpu.VMEM((2, ring, tok, width), bf16),
+            pltpu.VMEM((2, ring, tok, width), bf16),
+            pltpu.VMEM((2, 2, arm, tok, width), bf16),
+            pltpu.VMEM((2, 2, arm, tok, width), bf16),
+            dma((3,)),
+            dma((4, 2, arm)),
+            dma((4, 2, arm)),
+            dma((4, 2, arm + 1)),
+            dma((4, 2, arm + 1)),
+            dma((2, ring)),
+            dma((2, ring)),
+            dma((2, 2, arm)),
+            dma((2, 2, arm)),
+        ],
+        compiler_params=pltpu.CompilerParams(
+            collective_id=0, has_side_effects=True, vmem_limit_bytes=60 * 1024 * 1024
+        ),
+    )(forward_tokens, backward_tokens, backward_grad, route, gate_weight, up_weight, down_weight)
+
+
+def fits_fused(mesh, tokens_shape, ids_shape):
+    ep = mesh.shape["ep"]
+    tok = tokens_shape[0] // (ep * mesh.shape["rep"])
+    cap = tok * ids_shape[1] * 4 // (3 * ep)
+    held = ep * tok * tokens_shape[1] * 2
+    return ep % 4 == 0 and ep >= 12 and cap % 16 == 0 and 9 * held <= 36 * 1024 * 1024
+
+
 def solution(mesh):
-    in_specs = (
-        P(("rep", "ep"), None),
-        P(("rep", "ep"), None),
-        P(("rep", "ep"), None),
-        P(("rep", "ep"), None),
-        P(("rep", "ep"), None),
-        P(("rep", "ep"), None),
-        P(("rep", "ep"), None),
-        P(("rep", "ep"), None, None),
-        P(("rep", "ep"), None, None),
-        P(("rep", "ep"), None, None),
-    )
-    out_specs = (P(("rep", "ep"), None), P(("rep", "ep"), None))
-    return jax.shard_map(
-        per_device, mesh=mesh, in_specs=in_specs, out_specs=out_specs, check_vma=False
-    )
+    rows = P(("rep", "ep"), None)
+    stacked = P(("rep", "ep"), None, None)
+
+    def run(*args):
+        body = per_device_fused if fits_fused(mesh, args[0].shape, args[1].shape) else per_device
+        return jax.shard_map(
+            body, mesh=mesh, in_specs=(rows,) * 7 + (stacked,) * 3, out_specs=(rows, rows), check_vma=False
+        )(*args)
+
+    return run

time: 167 us -> 86.2 us (0.52); the launches traced: 165 us -> 85.8 us
  Pallas kernels: 0 us -> 75.7 us
  waiting for transfers between devices: 65.8 us -> 0 us
  starting transfers between devices: 34.6 us -> 0 us
  matrix products: 30.7 us -> 0 us
  local copies, waits for them, and re-layouts: 22.4 us -> 7.4 us
  other arithmetic: 10.4 us -> 2.07 us
    pallas_call x0 -> x1, Pallas kernels: none -> 75.7 us  [per_device_fused(): pl.pallas_call(functools.partial(fused_kernel, ep, cap), out_shape=(jax.S...]
    all_to_all x5 -> x0, waiting for transfers between devices: 65.8 us -> none  [the longest x1 21.4 us: per_device(): lax.all_to_all(sent_backward, 'ep', split_axis=0, concat_axis=0, tiled=True)]
    all_to_all x5 -> x0, starting transfers between devices: 34.6 us -> none  [the longest x1 7.41 us: per_device(): lax.all_to_all(sent_backward, 'ep', split_axis=0, concat_axis=0, tiled=True)]
    dot_general x9 -> x0, matrix products: 30.7 us -> none  [the longest x3 6.3 us: dispatch_rows(): jnp.dot(picker, values, preferred_element_type=jnp.float32)]
    gather x2 -> x0, local copies, waits for them, and re-layouts: 5.37 us -> none  [combine_rows(): picked = flat_rows[targets].astype(jnp.float32)]
    convert_element_type x2 -> x0, local copies, waits for them, and re-layouts: 5.11 us -> none  [combine_rows(): picked = flat_rows[targets].astype(jnp.float32)]
    unnamed x16 -> x6, local copies, waits for them, and re-layouts: 3.71 us -> 7.4 us
    another operation x4 -> x1, other arithmetic: 4.08 us -> 0.63 us  [per_device_fused(): jnp.stack([owner_weights(forward_ids, forward_mix, ep), owner_weights(bac...]
  transfers between devices with their start and end apart: 5 -> 0, of which waited for: 5 -> 0; matrix products, arithmetic and copies ran while one was open for 29% -> 0% of each run, Pallas kernels for 0% -> 0%
where the time goes in v1:
time: 86.2 us; the launch traced here: 85.8 us
  Pallas kernels  75.7 us (88%)
  local copies, waits for them, and re-layouts  7.4 us (9%)
  other arithmetic  2.07 us (2%)
    pallas_call x1, Pallas kernels, per_device_fused(): pl.pallas_call(functools.partial(fused_kernel, ep, cap), out_shape=(jax.S...  75.7 us
    unnamed x6, local copies, waits for them, and re-layouts  7.4 us

profile of v1, /device:TPU:0, one launch (start us, length us, event | category | flops | bytes accessed | tf_op | source)
XLA Modules:
  0.0 85.8 jit_solution(9635266204979096740)
XLA Ops:
  0.6 0.7 select_reduce_fusion.1
  1.3 0.7 select_reduce_fusion
  2.1 0.6 pad_maximum_fusion.rt_ref
  2.7 0.0 copy-start
  2.7 2.7 %copy.18.gate_hbm = bf16[1,1024,704]{2,1,0:T(8,128)(2,1)} copy(bf16[1,1024,704]{1,2,0:T(8,128)(2,1)} %param.17) | data formatting | bytes 2883584 | tf_op args[7]
  5.4 0.0 copy-done
  5.4 1.6 %copy.19.up_hbm = bf16[1,1024,704]{2,1,0:T(8,128)(2,1)} copy(bf16[1,1024,704]{1,2,0:T(8,128)(2,1)S(1)} %copy-done) | data formatting | bytes 2883584 | tf_op args[8]
  7.0 75.7 %shard_map.113 = (bf16[64,1024]{1,0:T(8,128)(2,1)}, bf16[64,1024]{1,0:T(8,128)(2,1)}) custom-call(bf16[64,1024]{1,0:T(8,128)(2,1)} %ft_ref.1, bf16[64,1024]{1,0:T(8,128)(2,1)} %bt_ref.1, bf16[64,1024]{1,0:T(8,128)(2,1)} %bg_ref.1, f32[16,2,64]{2,1,0:T(2,128)} %pad_maximum_fusion.rt_ref, bf16[1,1024,704]{2,1,0:T(8,128)(2,1)} %copy.18.gate_hbm, ...), custom_call_target="tpu_custom_call" | custom-call | tf_op jit(solution)/shard_map/pallas_call | solution.py:481
  82.7 1.6 %copy.22 = bf16[64,1024]{1,0:T(8,128)(2,1)} copy(bf16[64,1024]{1,0:T(8,128)(2,1)} %get-tuple-element.4) | data formatting | bytes 262144
  84.3 1.6 %copy.23 = bf16[64,1024]{1,0:T(8,128)(2,1)} copy(bf16[64,1024]{1,0:T(8,128)(2,1)} %get-tuple-element.5) | data formatting | bytes 262144
Async XLA Ops:
  2.7 2.7 %copy-start = (bf16[1,1024,704]{1,2,0:T(8,128)(2,1)S(1)}, bf16[1,1024,704]{1,2,0:T(8,128)(2,1)}, u32[]{:S(2)}) copy-start(bf16[1,1024,704]{1,2,0:T(8,128)(2,1)} %param.18) | copy-start | bytes 4325380

commit v2 on v1

--- a/solution.py
+++ b/solution.py
@@ -140,7 +140,10 @@
     ft_ref,
     bt_ref,
     bg_ref,
-    rt_ref,
+    fi_ref,
+    fm_ref,
+    bi_ref,
+    bm_ref,
     gate_hbm,
     up_hbm,
     down_hbm,
@@ -149,6 +152,7 @@
     bt_all,
     bg_all,
     ft_all,
+    rt_ref,
     rt_all,
     gate,
     up,
@@ -157,9 +161,11 @@
     mixrow,
     xrows,
     grows,
+    frows,
     zrows,
     pstage,
     precv,
+    psum,
     rstage,
     rrecv,
     wsem,
@@ -204,6 +210,15 @@
         copy.start()
         started.append(copy)
 
+    def table(ids_ref, mix_ref):
+        named = lax.broadcasted_iota(jnp.int32, (ep, tok), 0)
+        total = jnp.zeros((ep, tok), jnp.float32)
+        for k in range(ids_ref.shape[0]):
+            total = total + jnp.where(ids_ref[k : k + 1] == named, mix_ref[k : k + 1], 0.0)
+        return total
+
+    rt_ref[...] = jnp.concatenate([table(fi_ref, fm_ref), table(bi_ref, bm_ref)], axis=1)
+
     barrier = pltpu.get_barrier_semaphore()
     for other in (hop[0], hop[1], partner):
         pl.semaphore_signal(barrier, inc=1, device_id={"ep": other}, device_id_type=MESH_ID)
@@ -265,77 +280,89 @@
                 send_over(unit, way, dist)
 
     spot = lax.broadcasted_iota(jnp.int32, (cap, tok), 0).astype(jnp.float32)
-    earlier = (
-        lax.broadcasted_iota(jnp.int32, (tok, tok), 0) < lax.broadcasted_iota(jnp.int32, (tok, tok), 1)
-    ).astype(jnp.float32)
-
-    def choose(owner):
-        weights = rt_all[owner, me]
-        chosen = (weights > 0.0).astype(jnp.float32)
-        before = jnp.dot(chosen, earlier, preferred_element_type=jnp.float32)
+    first_at = lax.broadcasted_iota(jnp.int32, (2 * tok, 2 * tok), 0)
+    then_at = lax.broadcasted_iota(jnp.int32, (2 * tok, 2 * tok), 1)
+    earlier = ((first_at < then_at) & (first_at // tok == then_at // tok)).astype(jnp.float32)
+
+    slots = {(RIGHT, 0, 0): 0}
+    for dist in range(1, arm + 1):
+        for same, reach in ((0, dist), (1, dist - 1)):
+            for way in (RIGHT, LEFT):
+                if 0 < reach < arm or way == RIGHT:
+                    slots[way, reach, same] = len(slots)
+    slots[RIGHT, arm, 1] = len(slots)
+
+    def choose(owner, slot):
+        weights = rt_all[owner, pl.ds(me, 1)]
+        before = jnp.dot((weights > 0.0).astype(jnp.float32), earlier, preferred_element_type=jnp.float32)
         for kind in (FWD, BWD):
-            hit = (spot == before[kind : kind + 1]) & (weights[kind : kind + 1] > 0.0)
-            pick[kind, owner] = hit.astype(jnp.float32).astype(jnp.bfloat16)
-            scale = jnp.sum(jnp.where(hit, weights[kind : kind + 1], 0.0), axis=1, keepdims=True)
-            mixrow[kind, owner] = jnp.broadcast_to(scale, (cap, 128))
-
-    def fetch(kind, owner, source, rows):
-        rows[owner] = jnp.dot(
-            pick[kind, owner], source[owner], preferred_element_type=jnp.float32
+            lanes = slice(kind * tok, kind * tok + tok)
+            hit = (spot == before[:, lanes]) & (weights[:, lanes] > 0.0)
+            pick[kind, slot] = hit.astype(jnp.float32).astype(jnp.bfloat16)
+            scale = jnp.sum(jnp.where(hit, weights[:, lanes], 0.0), axis=1, keepdims=True)
+            mixrow[kind, slot] = jnp.broadcast_to(scale, (cap, 128))
+
+    def fetch(kind, owner, slot, source, rows):
+        rows[slot] = jnp.dot(
+            pick[kind, slot], source[owner], preferred_element_type=jnp.float32
         ).astype(jnp.bfloat16)
 
-    def take(kind, owner):
+    def take(kind, way, dist, same):
+        slot = slots[way, dist, same]
+        owner = owner_at(way, dist, core if same == 0 else 1 - core)
         if kind == BWD:
-            choose(owner)
-            fetch(BWD, owner, bt_all, xrows)
-            fetch(BWD, owner, bg_all, grows)
+            choose(owner, slot)
+            fetch(BWD, owner, slot, bt_all, xrows)
+            fetch(BWD, owner, slot, bg_all, grows)
         else:
-            fetch(FWD, owner, ft_all, xrows)
+            fetch(FWD, owner, slot, ft_all, frows)
 
     def take_ring(kind, dist):
-        take(kind, owner_at(RIGHT, dist, core))
-        if dist < arm:
-            take(kind, owner_at(LEFT, dist, core))
+        take(kind, RIGHT, dist, 0)
+        if 0 < dist < arm:
+            take(kind, LEFT, dist, 0)
 
     def take_over(kind, units, dist):
         ways = (RIGHT,) if dist == 0 else (RIGHT, LEFT)
         for unit in units:
             for way in ways:
                 await_over(unit, way, dist)
-        take(kind, owner_at(RIGHT, dist, 1 - core))
+        take(kind, RIGHT, dist, 1)
         if 0 < dist < arm:
-            take(kind, owner_at(LEFT, dist, 1 - core))
-
-    span = ep // 2
-
-    def scaled(kind, first, value):
-        scale = mixrow[kind, pl.ds(first, span)].reshape(span * cap, 128)[:, :1]
-        zrows[kind, pl.ds(first, span)] = (value * scale).astype(jnp.bfloat16).reshape(span, cap, width)
+            take(kind, LEFT, dist, 1)
+
+    def scaled(kind, first, span, value):
+        scale = mixrow[kind, first : first + span].reshape(span * cap, 128)[:, :1]
+        zrows[kind, first : first + span] = (value * scale).astype(jnp.bfloat16).reshape(span, cap, width)
 
     def nt(left, right):
         return lax.dot_general(left, right, (((1,), (1,)), ((), ())), preferred_element_type=jnp.float32)
 
-    def expert_b(first):
-        x = xrows[pl.ds(first, span)].reshape(span * cap, width)
-        g = grows[pl.ds(first, span)].reshape(span * cap, width)
-        p = jnp.dot(x, gate[...], preferred_element_type=jnp.float32)
-        q = jnp.dot(x, up[...], preferred_element_type=jnp.float32)
+    def nn(left, right):
+        return jnp.dot(left, right, preferred_element_type=jnp.float32)
+
+    def expert_b(first, span):
+        x = xrows[first : first + span].reshape(span * cap, width)
+        g = grows[first : first + span].reshape(span * cap, width)
+        p = nt(x, gate[...])
+        q = nt(x, up[...])
         hidden_grad = nt(g, down[...])
         s = jax.nn.sigmoid(p)
         gate_grad = (hidden_grad * q * s * (1.0 + p * (1.0 - s))).astype(jnp.bfloat16)
         up_grad = (hidden_grad * p * s).astype(jnp.bfloat16)
-        scaled(BWD, first, nt(gate_grad, gate[...]) + nt(up_grad, up[...]))
-
-    def expert_f(first):
-        x = xrows[pl.ds(first, span)].reshape(span * cap, width)
-        p = jnp.dot(x, gate[...], preferred_element_type=jnp.float32)
-        q = jnp.dot(x, up[...], preferred_element_type=jnp.float32)
+        scaled(BWD, first, span, nn(gate_grad, gate[...]) + nn(up_grad, up[...]))
+
+    def expert_f(first, span):
+        x = frows[first : first + span].reshape(span * cap, width)
+        p = nt(x, gate[...])
+        q = nt(x, up[...])
         hidden = (p * jax.nn.sigmoid(p) * q).astype(jnp.bfloat16)
-        scaled(FWD, first, jnp.dot(hidden, down[...], preferred_element_type=jnp.float32))
-
-    def contribution(kind, owner):
+        scaled(FWD, first, span, nn(hidden, down[...]))
+
+    def contribution(kind, j, same):
+        slot = slots[(RIGHT, ring - j, same) if j >= arm else (LEFT if j else RIGHT, j, same)]
         return lax.dot_general(
-            pick[kind, owner], zrows[kind, owner], (((0,), (0,)), ((), ())), preferred_element_type=jnp.float32
+            pick[kind, slot], zrows[kind, slot], (((0,), (0,)), ((), ())), preferred_element_type=jnp.float32
         )
 
     order = [arm] + [j for d in range(arm - 1, 0, -1) for j in (d, ring - d)] + [0]
@@ -343,52 +370,63 @@
     def pair_copy(kind, j):
         return remote(pstage.at[kind, j], precv.at[kind, j], ps_send.at[kind, j], ps_recv.at[kind, j], partner)
 
-    def hand_over(kind):
-        for j in order:
-            pstage[kind, j] = contribution(kind, member(j, 1 - core)).astype(jnp.bfloat16)
+    def hand_over(kind, places):
+        for j in places:
+            pstage[kind, j] = contribution(kind, j, 1).astype(jnp.bfloat16)
             launch(pair_copy(kind, j))
 
-    def pair_sum(kind, j):
+    def add_pair(kind, j):
+        value = contribution(kind, j, 0)
         pair_copy(kind, j).wait_recv()
-        return contribution(kind, member(j, core)) + precv[kind, j].astype(jnp.float32)
-
-    def ring_copy(kind, way, step):
-        src, dst = rstage.at[kind, way, step], rrecv.at[kind, way, step]
-        if step == 0:
-            src, dst = src.at[pl.ds(half * way, half)], dst.at[pl.ds(half * way, half)]
-        return remote(src, dst, rs_send.at[kind, way, step], rs_recv.at[kind, way, step], hop[way])
-
-    def reduce_step(kind, step):
-        dist = arm - step
-        if step == 0:
-            value = pair_sum(kind, arm).astype(jnp.bfloat16)
+        psum[kind, j] = value + precv[kind, j].astype(jnp.float32)
+
+    def ring_copy(kind, way, piece, dist):
+        at = (kind, way, dist - 1, pl.ds(half * piece, half))
+        return remote(rstage.at[at], rrecv.at[at], rs_send.at[kind, way, piece, dist - 1],
+                      rs_recv.at[kind, way, piece, dist - 1], hop[way])
+
+    def reach(way, piece):
+        return arm if piece == way else arm - 1
+
+    def pass_on(kind, way, piece, dist):
+        rows = pl.ds(half * piece, half)
+        value = psum[kind, dist if way == RIGHT else ring - dist, rows]
+        if dist < reach(way, piece):
+            ring_copy(kind, way, piece, dist + 1).wait_recv()
+            value = value + rrecv[kind, way, dist, rows].astype(jnp.float32)
+        rstage[kind, way, dist - 1, rows] = value.astype(jnp.bfloat16)
+        launch(ring_copy(kind, way, piece, dist))
+
+    def reduce_at(kind, dist):
+        for lead in (True, False):
             for way in (RIGHT, LEFT):
-                rows = pl.ds(half * way, half)
-                rstage[kind, way, 0, rows] = value[half * way : half * way + half]
-                launch(ring_copy(kind, way, 0))
-            return
+                piece = way if lead else 1 - way
+                if dist <= reach(way, piece):
+                    pass_on(kind, way, piece, dist)
+
+    def prepare(kind, dist):
+        for j in (dist,) if dist in (0, arm) else (dist, ring - dist):
+            add_pair(kind, j)
+
+    def open_chains(kind):
+        prepare(kind, arm)
+        reduce_at(kind, arm)
+        prepare(kind, arm - 1)
         for way in (RIGHT, LEFT):
-            value = pair_sum(kind, dist if way == RIGHT else ring - dist)
-            ring_copy(kind, way, step - 1).wait_recv()
-            if step == 1:
-                for at in (RIGHT, LEFT):
-                    piece = value[half * at : half * at + half]
-                    rows = pl.ds(half * at, half)
-                    if at == way:
-                        piece = piece + rrecv[kind, way, 0, rows].astype(jnp.float32)
-                    rstage[kind, way, 1, rows] = piece.astype(jnp.bfloat16)
-            else:
-                rstage[kind, way, step] = (value + rrecv[kind, way, step - 1].astype(jnp.float32)).astype(
-                    jnp.bfloat16
-                )
-            launch(ring_copy(kind, way, step))
+            pass_on(kind, way, 1 - way, arm - 1)
+
+    def second(kind):
+        for way in (RIGHT, LEFT):
+            pass_on(kind, way, way, arm - 1)
 
     def finish(kind, out_ref):
-        value = pair_sum(kind, 0)
-        for way in (RIGHT, LEFT):
-            ring_copy(kind, way, arm - 1).wait_recv()
-            value = value + rrecv[kind, way, arm - 1].astype(jnp.float32)
-        out_ref[...] = value.astype(jnp.bfloat16)
+        for piece in (0, 1):
+            rows = pl.ds(half * piece, half)
+            value = psum[kind, 0, rows]
+            for way in (RIGHT, LEFT):
+                ring_copy(kind, way, piece, 1).wait_recv()
+                value = value + rrecv[kind, way, 0, rows].astype(jnp.float32)
+            out_ref[rows] = value.astype(jnp.bfloat16)
 
     units_b = (ROUTE, TOK_B, GRAD_B)
     units_f = (TOK_F,)
@@ -401,56 +439,68 @@
         load.start()
     for unit in range(4):
         gathered[unit][me] = sources[unit][...]
-    take(BWD, me)
+    take(BWD, RIGHT, 0, 0)
+    done = 0
     for dist in range(1, arm + 1):
         forward(units_b, dist)
         if dist == arm - 1:
             begin(units_f)
-        if dist < arm:
-            take_ring(BWD, dist)
+        take_ring(BWD, dist)
         take_over(BWD, units_b, dist - 1)
-    take_ring(BWD, arm)
+        if dist == 2:
+            for load in loads:
+                load.wait()
+        if 2 <= dist < arm:
+            ready = 4 * dist
+            expert_b(done, ready - done)
+            done = ready
     take_over(BWD, units_b, arm)
-    for load in loads:
-        load.wait()
     forward(units_f, 1)
-    expert_b(0)
-    if arm >= 2:
-        forward(units_f, 2)
-    expert_b(span)
-    for dist in range(3, arm + 1):
-        if dist < arm:
-            forward(units_f, dist)
-    hand_over(BWD)
-    reduce_step(BWD, 0)
-    if arm >= 3:
-        forward(units_f, arm)
-    take(FWD, me)
-    for dist in range(1, arm):
-        take_ring(FWD, dist)
-    reduce_step(BWD, 1)
+    expert_b(done, ep - done)
+    hand_over(BWD, order[:3])
+    take(FWD, RIGHT, 0, 0)
+    take_ring(FWD, 1)
+    take_over(FWD, units_f, 0)
+    forward(units_f, 2)
+    open_chains(BWD)
+    hand_over(BWD, order[3:])
+    take_ring(FWD, 2)
+    take_over(FWD, units_f, 1)
+    for dist in range(arm - 2, -1, -1):
+        prepare(BWD, dist)
+    forward(units_f, 3)
+    second(BWD)
+    expert_f(0, 8)
+    done = 8
+    for dist in range(4, arm + 1):
+        take_ring(FWD, dist - 1)
+        take_over(FWD, units_f, dist - 2)
+        forward(units_f, dist)
+        reduce_at(BWD, arm - dist + 2)
+        expert_f(done, 4)
+        done += 4
     take_ring(FWD, arm)
-    for dist in range(0, arm + 1):
-        take_over(FWD, units_f, dist)
-    expert_f(0)
-    for step in range(2, arm - 1):
-        reduce_step(BWD, step)
-    expert_f(span)
-    if arm >= 3:
-        reduce_step(BWD, arm - 1)
-    hand_over(FWD)
-    reduce_step(FWD, 0)
+    take_over(FWD, units_f, arm - 1)
+    take_over(FWD, units_f, arm)
+    expert_f(done, ep - done)
+    reduce_at(BWD, 1)
+    hand_over(FWD, order[:3])
+    open_chains(FWD)
+    hand_over(FWD, order[3:])
+    for dist in range(arm - 2, -1, -1):
+        prepare(FWD, dist)
+    second(FWD)
     finish(BWD, ob_ref)
-    for step in range(1, arm):
-        reduce_step(FWD, step)
+    for dist in range(arm - 2, 0, -1):
+        reduce_at(FWD, dist)
     finish(FWD, of_ref)
     for copy in started:
         copy.wait_send()
 
 
-def owner_weights(ids, mix, experts):
-    named = ids[None, :, :] == jnp.arange(experts, dtype=jnp.int32)[:, None, None]
-    return jnp.sum(jnp.where(named, mix[None, :, :], 0.0), axis=2)
+def settle_kernel(forward_ref, backward_ref, forward_out, backward_out):
+    forward_out[...] = forward_ref[...]
+    backward_out[...] = backward_ref[...]
 
 
 def per_device_fused(
@@ -472,30 +522,30 @@
     ring = ep // 2
     arm = ring // 2
     bf16, f32 = jnp.bfloat16, jnp.float32
-    route = jnp.stack(
-        [owner_weights(forward_ids, forward_mix, ep), owner_weights(backward_ids, backward_mix, ep)], axis=1
-    )
     vmem = pl.BlockSpec(memory_space=pltpu.VMEM)
     hbm = pl.BlockSpec(memory_space=pl.ANY)
     dma = pltpu.SemaphoreType.DMA
-    return pl.pallas_call(
+    results = pl.pallas_call(
         functools.partial(fused_kernel, ep, cap),
         out_shape=(jax.ShapeDtypeStruct((tok, width), bf16),) * 2,
-        in_specs=[vmem] * 4 + [hbm] * 3,
+        in_specs=[vmem] * 7 + [hbm] * 3,
         out_specs=(vmem, vmem),
         scratch_shapes=[pltpu.VMEM((ep, tok, width), bf16)] * 3
         + [
-            pltpu.VMEM((ep, ep, 2, tok), f32),
-            pltpu.VMEM(gate_weight.shape[1:], bf16),
-            pltpu.VMEM(up_weight.shape[1:], bf16),
+            pltpu.VMEM((ep, 2 * tok), f32),
+            pltpu.VMEM((ep, ep, 2 * tok), f32),
+            pltpu.VMEM(gate_weight.shape[:0:-1], bf16),
+            pltpu.VMEM(up_weight.shape[:0:-1], bf16),
             pltpu.VMEM(down_weight.shape[1:], bf16),
             pltpu.VMEM((2, ep, cap, tok), bf16),
             pltpu.VMEM((2, ep, cap, 128), f32),
             pltpu.VMEM((ep, cap, width), bf16),
             pltpu.VMEM((ep, cap, width), bf16),
+            pltpu.VMEM((ep, cap, width), bf16),
             pltpu.VMEM((2, ep, cap, width), bf16),
             pltpu.VMEM((2, ring, tok, width), bf16),
             pltpu.VMEM((2, ring, tok, width), bf16),
+            pltpu.VMEM((2, ring, tok, width), f32),
             pltpu.VMEM((2, 2, arm, tok, width), bf16),
             pltpu.VMEM((2, 2, arm, tok, width), bf16),
             dma((3,)),
@@ -505,13 +555,32 @@
             dma((4, 2, arm + 1)),
             dma((2, ring)),
             dma((2, ring)),
-            dma((2, 2, arm)),
-            dma((2, 2, arm)),
+            dma((2, 2, 2, arm)),
+            dma((2, 2, 2, arm)),
         ],
         compiler_params=pltpu.CompilerParams(
             collective_id=0, has_side_effects=True, vmem_limit_bytes=60 * 1024 * 1024
         ),
-    )(forward_tokens, backward_tokens, backward_grad, route, gate_weight, up_weight, down_weight)
+    )(
+        forward_tokens,
+        backward_tokens,
+        backward_grad,
+        forward_ids.T,
+        forward_mix.T,
+        backward_ids.T,
+        backward_mix.T,
+        gate_weight.swapaxes(1, 2),
+        up_weight.swapaxes(1, 2),
+        down_weight,
+    )
+    return tuple(
+        pl.pallas_call(
+            settle_kernel,
+            out_shape=(jax.ShapeDtypeStruct((tok, width), bf16),) * 2,
+            in_specs=[vmem] * 2,
+            out_specs=(vmem, vmem),
+        )(*results)
+    )
 
 
 def fits_fused(mesh, tokens_shape, ids_shape):
@@ -519,7 +588,7 @@
     tok = tokens_shape[0] // (ep * mesh.shape["rep"])
     cap = tok * ids_shape[1] * 4 // (3 * ep)
     held = ep * tok * tokens_shape[1] * 2
-    return ep % 4 == 0 and ep >= 12 and cap % 16 == 0 and 9 * held <= 36 * 1024 * 1024
+    return ep % 4 == 0 and ep >= 16 and cap % 16 == 0 and 11 * held <= 36 * 1024 * 1024
 
 
 def solution(mesh):

time: 86.2 us -> 72.2 us (0.84)
  local copies, waits for them, and re-layouts: 7.4 us -> 0 us
  Pallas kernels: 75.7 us -> 71.4 us
  other arithmetic: 2.07 us -> 0 us
    unnamed x6 -> x0, local copies, waits for them, and re-layouts: 7.4 us -> none
    pallas_call x1, Pallas kernels: 75.7 us -> 69.8 us  [per_device_fused(): pl.pallas_call(functools.partial(fused_kernel, ep, cap), out_shape=(jax.S...]
    pallas_call x0 -> x1, Pallas kernels: none -> 1.68 us  [per_device_fused(): pl.pallas_call(settle_kernel, out_shape=(jax.ShapeDtypeStruct((tok, width...]
    reduce_sum x2 -> x0, other arithmetic: 1.44 us -> none  [owner_weights(): return jnp.sum(jnp.where(named, mix[None, :, :], 0.0), axis=2)]
where the time goes in v2:
time: 72.2 us; the launch traced here: 72.1 us
  Pallas kernels  71.4 us (99%)
    pallas_call x1, Pallas kernels, per_device_fused(): pl.pallas_call(functools.partial(fused_kernel, ep, cap), out_shape=(jax.S...  69.8 us
    pallas_call x1, Pallas kernels, per_device_fused(): pl.pallas_call(settle_kernel, out_shape=(jax.ShapeDtypeStruct((tok, width...  1.68 us

profile of v2, /device:TPU:0, one launch (start us, length us, event | category | flops | bytes accessed | tf_op | source)
XLA Modules:
  0.0 72.1 jit_solution(452831073075682477)
XLA Ops:
  0.6 69.8 %shard_map.113 = (bf16[64,1024]{1,0:T(8,128)(2,1)}, bf16[64,1024]{1,0:T(8,128)(2,1)}) custom-call(bf16[64,1024]{1,0:T(8,128)(2,1)} %ft_ref.1, bf16[64,1024]{1,0:T(8,128)(2,1)} %bt_ref.1, bf16[64,1024]{1,0:T(8,128)(2,1)} %bg_ref.1, s32[6,64]{1,0:T(8,128)} %bitcast.8, f32[6,64]{1,0:T(8,128)} %bitcast.9, s32[6,64]{1,0:T(8,128)} %bitcast.10, f32[6,64]{1,0:T(8,128)} %bitcast.11, ...), custom_call_target="tpu_custom_call" | custom-call | tf_op jit(solution)/shard_map/pallas_call | solution.py:528
  70.4 1.7 %shard_map.114 = (bf16[64,1024]{1,0:T(8,128)(2,1)}, bf16[64,1024]{1,0:T(8,128)(2,1)}) custom-call(bf16[64,1024]{1,0:T(8,128)(2,1)} %get-tuple-element.4.forward_ref, bf16[64,1024]{1,0:T(8,128)(2,1)} %get-tuple-element.5.backward_ref), custom_call_target="tpu_custom_call" | custom-call | tf_op jit(solution)/shard_map/pallas_call | solution.py:577
